TPU v7x, 256 devices: a whole 4x4x8 slice. The times are simulated.
256 devices in a mesh: samp: 4 (over y), snp: 64 (over z, x, core).
Axes of the slice: x: 4, y: 4, z: 8, core: 2. Of those that a mesh axis runs over, the one named last changes fastest.
Arguments:
- genotypes: int32 [8192, 65536], P('samp', 'snp'), may hold values from 0 to 2
- win_lo: int32 [65536], P('snp'), may hold values from 0 to 65535, as said below
- win_hi: int32 [65536], P('snp'), may hold values from 0 to 65535, as said below
- annotation: int32 [65536], P('snp'), may hold values from 0 to 127
- chromosome: int32 [65536], P('snp'), may hold values from 0 to 21, never falling along the last dimension, each value on 1 to 4096 neighbouring positions
- chi_square: float32 [65536], P('snp'), may hold values from 0.3 to 60
Outputs:
- annotation_scores: float32 [128, 65536], P('snp')
- gram: float32 [128, 128], replicated
- moments: float32 [2, 128], replicated
- totals: float32 [2], replicated
Inputs may be any that keep to these rules, and one draw needn't show every extreme that they name: i - 512 <= win_lo[i] <= i, nondecreasing in i; the distance 512 is reached. i <= win_hi[i] <= i + 512, nondecreasing in i; the distance 512 is reached.
All inputs are finite; a program needn't handle non-finite values.
Results may differ from a plain program's by a relative error of at most 0.0003.
The roundings to bfloat16 on the way count: a program that leaves them out, or rounds other values in their place, can miss the bound.
Values may be sent and summed in bfloat16 or wider, within the bound.
No kernel may reach another device: no remote copies, remote signals or barrier semaphores. Data moves between devices by JAX's collectives and lax.ppermute only.
A program may use at most 64 MiB of HBM per device.

v0:
```python
import jax
import jax.numpy as jnp
from jax import lax
from jax.sharding import PartitionSpec as P

A = 128


def from_everyone(array, axis):
    size = lax.axis_size(axis)
    return lax.all_to_all(
        jnp.broadcast_to(array[None], (size, *array.shape)), axis, 0, 0, tiled=True
    )


def of_everyone(array, axis):
    return from_everyone(array, axis).sum(axis=0)


def packed_total(arrays, axis):
    flat, at, finished = (jnp.concatenate([a.reshape(-1) for a in arrays]), 0, [])
    so_far = of_everyone(flat, axis)
    for a in arrays:
        finished.append(so_far[at : at + a.size].reshape(a.shape))
        at += a.size
    return tuple(finished)


def extended(cells, sides, width):
    for axis, dim in sides:
        count = lax.axis_size(axis)
        ends = count - 1
        head = lax.slice_in_dim(cells, 0, width, axis=dim)
        tail = lax.slice_in_dim(cells, cells.shape[dim] - width, cells.shape[dim], axis=dim)
        cells = jnp.concatenate(
            [
                lax.ppermute(tail, axis, [(i, (i + 1) % count) for i in range(ends)]),
                cells,
                lax.ppermute(head, axis, [((i + 1) % count, i) for i in range(ends)]),
            ],
            axis=dim,
        )
    return cells


def cut_along(array, dim, size):
    dims = array.shape
    pieces = array.reshape(*dims[:dim], size, dims[dim] // size, *dims[dim + 1 :])
    return jnp.moveaxis(pieces, dim, 0)


def sum_at_owner(array, axis, dim):
    pieces = cut_along(array, dim, lax.axis_size(axis))
    arrived = lax.all_to_all(pieces, axis, split_axis=0, concat_axis=0, tiled=True)
    return arrived.sum(axis=0)


def rows_for(lines, size):
    spare = -lines.shape[0] % size
    if not spare:
        return lines
    return jnp.concatenate([lines, jnp.zeros((spare, *lines.shape[1:]), lines.dtype)])


def laid_out(pieces, dim):
    dims = list(pieces.shape[1:])
    dims[dim] *= pieces.shape[0]
    return jnp.moveaxis(pieces, 0, dim).reshape(dims)


def collect(array, axis, dim):
    pieces = from_everyone(array, axis)
    return laid_out(pieces, dim)


def total_of(array, axes):
    own = sum_at_owner(rows_for(array, lax.axis_size(axes)), axes, 0)
    whole = collect(own, axes, 0)
    return whole[: len(array)].reshape(array.shape)


def in_one(arrays, axis):
    ends = [0]
    for a in arrays:
        ends.append(ends[-1] + a.size)
    so_far = total_of(jnp.concatenate([a.ravel() for a in arrays]), axis)
    return tuple((so_far[b:e].reshape(a.shape) for a, b, e in zip(arrays, ends, ends[1:])))


def body(genotypes, win_lo, win_hi, annotation, chromosome, chi_square):
    samp_rows, block_cols = genotypes.shape
    reach = block_cols // 2
    samp_count = lax.axis_size("samp")
    total_samples = samp_rows * samp_count
    dosage = genotypes.astype(jnp.float32)
    dose_sums, dose_squares = packed_total(
        (jnp.sum(dosage, 0), jnp.sum(dosage * dosage, 0)), "samp"
    )
    mean_dose = dose_sums / total_samples
    variance = dose_squares / total_samples - mean_dose * mean_dose
    standard = ((dosage - mean_dose) * lax.rsqrt(variance + 1e-05)).astype(jnp.bfloat16)
    first_snp = lax.axis_index("snp") * block_cols
    labels = jnp.arange(A, dtype=jnp.int32)
    own_labels = jnp.stack([annotation, chromosome]).astype(jnp.bfloat16)
    wide_z, wide_labels = (
        extended(standard, (("snp", 1),), reach),
        extended(own_labels, (("snp", 1),), reach),
    )
    annot_wide = wide_labels[0].astype(jnp.int32)
    chrom_wide = wide_labels[1].astype(jnp.int32)
    span = wide_z.shape[1] - block_cols + reach

    def tile_piece(row_start, count):
        band = row_start // reach * reach
        rows_z = lax.dynamic_slice_in_dim(standard, row_start, count, 1)
        cols_z = lax.dynamic_slice_in_dim(wide_z, band, span, 1)
        return lax.dot_general(
            rows_z, cols_z, (((0,), (0,)), ((), ())), preferred_element_type=jnp.float32
        )

    share = block_cols // samp_count
    row_start = jnp.int32(0)
    tile = sum_at_owner(
        jnp.concatenate(
            [
                tile_piece(row_start + offset * share, share)
                for offset in range(share * lax.axis_size("samp") // share)
            ],
            0,
        ),
        "samp",
        0,
    )
    row_begin = lax.axis_index("samp") * share
    row_start = row_begin + 0
    band = row_start // reach * reach
    corr = tile / total_samples
    square = corr * corr
    adjusted = square - (1.0 - square) / (total_samples - 2)
    col_ids = first_snp + band - reach + jnp.arange(span, dtype=jnp.int32)
    lower_end = lax.dynamic_slice_in_dim(win_lo, row_start, share)
    upper_end = lax.dynamic_slice_in_dim(win_hi, row_start, share)
    chrom_rows = lax.dynamic_slice_in_dim(chromosome, row_start, share)
    chrom_cols = lax.dynamic_slice_in_dim(chrom_wide, band, span)
    annot_cols = lax.dynamic_slice_in_dim(annot_wide, band, span)
    inside = (col_ids[None, :] >= lower_end[:, None]) & (col_ids[None, :] <= upper_end[:, None])
    inside = inside & (chrom_cols[None, :] == chrom_rows[:, None])
    kept = jnp.where(inside, adjusted, 0.0)
    member = (annot_cols[:, None] == labels[None, :]).astype(jnp.float32)
    part_scores = lax.dot_general(
        member,
        kept,
        (((0,), (1,)), ((), ())),
        precision=lax.Precision.HIGHEST,
        preferred_element_type=jnp.float32,
    )
    scores = lax.all_gather(part_scores, "samp", axis=1, tiled=True)
    weights = 1.0 / jnp.sum(scores, 0)
    weighted = scores * weights[None, :]
    gram_part = lax.dot_general(
        weighted,
        scores,
        (((1,), (1,)), ((), ())),
        precision=lax.Precision.HIGHEST,
        preferred_element_type=jnp.float32,
    )
    moment_part = jnp.stack([jnp.sum(weighted, 1), jnp.sum(weighted * chi_square[None, :], 1)])
    total_part = jnp.stack([jnp.sum(weights), jnp.sum(weights * chi_square)])
    gram, moments, totals = in_one((gram_part, moment_part, total_part), "snp")
    snp_total = block_cols * lax.axis_size("snp")
    scale = A / snp_total
    regrouped = lax.all_to_all(scores, "snp", split_axis=0, concat_axis=1, tiled=True)
    return (regrouped, scale * gram, scale * moments, totals / snp_total)


def solution(mesh):
    in_specs = (P("samp", "snp"), P("snp"), P("snp"), P("snp"), P("snp"), P("snp"))
    out_specs = (P("snp", None), P(), P(), P())
    return jax.shard_map(body, mesh=mesh, in_specs=in_specs, out_specs=out_specs, check_vma=False)
```

profile of v0, /device:TPU:1, one launch (start us, length us, event | category | flops | bytes accessed | tf_op | source)
XLA Modules:
  0.0 217.3 jit_solution(6880136489920575053)
XLA Ops:
  0.6 4.5 %convert_reduce_fusion = (f32[1024]{0:T(1024)S(1)}, f32[1024]{0:T(1024)S(1)}) fusion(s32[2048,1024]{1,0:T(8,128)} %param.6), kind=kLoop, calls=%fused_computation.2 | loop fusion | flops 8386560 | bytes 8396800 | tf_op jit(solution)/shard_map/reduce_sum | solution.py:97
  5.2 9.1 %all_to_all.45 = f32[4,1,2048]{2,1,0:T(1,128)S(1)} all-to-all(f32[4,1,2048]{2,1,0:T(1,128)S(1)} %broadcast_in_dim.9), channel_id=1, replica_groups=mesh['samp'=4,'snp'=64] {'samp'}, dimensions={0} | all-to-all | bytes 65536 | tf_op jit(solution)/shard_map/all_to_all | solution.py:11
  14.4 4.7 %multiply_convert_fusion = bf16[2048,1024]{1,0:T(8,128)(2,1)S(1)} fusion(s32[2048,1024]{1,0:T(8,128)} %param.6, f32[1024]{0:T(1024)S(1)} %get-tuple-element.17, f32[1024]{0:T(1024)S(1)} %get-tuple-element.16), kind=kLoop, calls=%fused_computation | loop fusion | flops 8388608 | bytes 12591104 | tf_op jit(solution)/shard_map/convert_element_type | solution.py:101
  19.4 4.0 %collective-permute-start.3 = (bf16[2048,512]{1,0:T(8,128)(2,1)S(1)}, bf16[2048,512]{1,0:T(8,128)(2,1)S(1)}, u32[]{:S(2)}, u32[]{:S(2)}) collective-permute-start(bf16[2048,512]{1,0:T(8,128)(2,1)S(1)} %get-tuple-element.11), channel_id=1, source_target_pairs={{1,0},{2,1},{3,2},{4,3},{5,4},{6,5},{7,6},{8,7},{9,8},{10,9},{11,1... | collective-permute-start | bytes 6291464 | tf_op jit(solution)/shard_map/ppermute | solution.py:39
  23.4 3.0 %collective-permute-start.2 = (bf16[2048,512]{1,0:T(8,128)(2,1)S(1)}, bf16[2048,512]{1,0:T(8,128)(2,1)S(1)}, u32[]{:S(2)}, u32[]{:S(2)}) collective-permute-start(bf16[2048,512]{1,0:T(8,128)(2,1)S(1)} %get-tuple-element.10), channel_id=1, source_target_pairs={{0,1},{1,2},{2,3},{3,4},{4,5},{5,6},{6,7},{7,8},{8,9},{9,10},{10,1... | collective-permute-start | bytes 6291464 | tf_op jit(solution)/shard_map/ppermute | solution.py:37
  26.4 22.2 %collective-permute-done.3 = bf16[2048,512]{1,0:T(8,128)(2,1)S(1)} collective-permute-done((bf16[2048,512]{1,0:T(8,128)(2,1)S(1)}, bf16[2048,512]{1,0:T(8,128)(2,1)S(1)}, u32[]{:S(2)}, u32[]{:S(2)}) %collective-permute-start.3) | collective-permute-done | bytes 2097184 | tf_op jit(solution)/shard_map/ppermute | solution.py:39
  48.6 1.8 fusion
  50.4 1.8 fusion.1
  52.2 1.8 fusion.2
  54.0 1.8 fusion.3
  55.9 3.0 %pad_maximum_fusion.2 = f32[1024,1536]{1,0:T(8,128)} fusion(f32[256,1536]{1,0:T(8,128)S(1)} %fusion, f32[256,1536]{1,0:T(8,128)S(1)} %fusion.1, f32[256,1536]{1,0:T(8,128)S(1)} %fusion.2, f32[256,1536]{1,0:T(8,128)S(1)} %fusion.3), kind=kLoop, calls=%fused_computation.5 | loop fusion | flops 4718592 | bytes 12582912 | tf_op jit(solution)/shard_map/concatenate | solution.py:124
  58.9 5.4 %all-to-all-start.1 = ((f32[4,256,1536]{2,1,0:T(8,128)}), f32[4,256,1536]{2,1,0:T(8,128)}, u32[]{:S(2)}, u32[]{:S(2)}) async-start(f32[4,256,1536]{2,1,0:T(8,128)} %bitcast.17), calls=%async_computation.1 | async-start | bytes 12582912 | tf_op jit(solution)/shard_map/all_to_all | solution.py:54
  64.3 1.9 collective-permute-start.1
  66.3 3.8 %collective-permute-start = (bf16[2,512]{1,0:T(2,128)(2,1)S(1)}, bf16[2,512]{1,0:T(2,128)(2,1)S(1)}, u32[]{:S(2)}, u32[]{:S(2)}) collective-permute-start(bf16[2,512]{1,0:T(2,128)(2,1)S(1)} %get-tuple-element.14), channel_id=1, source_target_pairs={{0,1},{1,2},{2,3},{3,4},{4,5},{5,6},{6,7},{7,8},{8,9},{9,10},{10,1... | collective-permute-start | bytes 6152 | tf_op jit(solution)/shard_map/ppermute | solution.py:37
  70.2 0.8 dynamic_slice.38
  71.0 0.8 dynamic_slice.37
  71.8 44.8 %all-to-all-done.1 = f32[4,256,1536]{2,1,0:T(8,128)} async-done(((f32[4,256,1536]{2,1,0:T(8,128)}), f32[4,256,1536]{2,1,0:T(8,128)}, u32[]{:S(2)}, u32[]{:S(2)}) %all-to-all-start.1) | async-done | bytes 6291488 | tf_op jit(solution)/shard_map/all_to_all | solution.py:54
  116.7 3.6 %reduce_sum.93 = f32[256,1536]{1,0:T(8,128)S(1)} reduce(f32[4,256,1536]{2,1,0:T(8,128)} %all-to-all-done.1, f32[]{:T(128)} %constant.123.clone.1), dimensions={0}, to_apply=%region_3.4 | reduce | flops 1179648 | bytes 7864324 | tf_op jit(solution)/shard_map/reduce_sum | solution.py:55
  120.2 1.6 fusion.4
  121.9 9.9 %all_gather.3 = f32[128,1024]{1,0:T(8,128)S(1)} all-gather(f32[128,256]{1,0:T(8,128)S(1)} %fusion.4), channel_id=1, replica_groups=mesh['samp'=4,'snp'=64] {'samp'}, dimensions={1}, use_global_device_ids=true | all-gather | bytes 655360 | tf_op jit(solution)/shard_map/all_gather | solution.py:157
  131.8 0.6 multiply_reduce_fusion.2
  132.4 0.6 convolution_bitcast_fusion
  133.2 1.4 concatenate.24
  134.9 43.4 %all_to_all.46 = f32[64,1,261]{2,1,0:T(1,128)S(1)} all-to-all(f32[64,1,261]{2,1,0:T(1,128)S(1)} %all_to_all.37), channel_id=1, replica_groups=mesh['samp'=4,'snp'=64] {'snp'}, dimensions={0} | all-to-all | bytes 133632 | tf_op jit(solution)/shard_map/all_to_all | solution.py:54
  178.4 0.7 broadcast_in_dim.12
  179.0 4.4 %all-to-all-start.4 = ((f32[64,1,261]{2,1,0:T(1,128)}), f32[64,1,261]{2,1,0:T(1,128)S(1)}, u32[]{:S(2)}, u32[]{:S(2)}) async-start(f32[64,1,261]{2,1,0:T(1,128)} %broadcast_in_dim.12), calls=%async_computation.4 | async-start | bytes 196608 | tf_op jit(solution)/shard_map/all_to_all | solution.py:11
  183.5 1.1 all_to_all.33
  184.6 9.6 %all-to-all-done.4 = f32[64,1,261]{2,1,0:T(1,128)S(1)} async-done(((f32[64,1,261]{2,1,0:T(1,128)}), f32[64,1,261]{2,1,0:T(1,128)S(1)}, u32[]{:S(2)}, u32[]{:S(2)}) %all-to-all-start.4) | async-done | bytes 66848 | tf_op jit(solution)/shard_map/all_to_all | solution.py:11
  194.2 4.5 %all-to-all-start.2 = ((f32[64,2,1024]{2,1,0:T(2,128)}), f32[64,2,1024]{2,1,0:T(2,128)S(1)}, u32[]{:S(2)}, u32[]{:S(2)}) async-start(f32[64,2,1024]{2,1,0:T(2,128)} %all_to_all.33), calls=%async_computation.2 | async-start | bytes 1048576 | tf_op jit(solution)/shard_map/all_to_all | solution.py:172
  200.2 0.6 fusion.35
  200.8 15.6 %all-to-all-done.2 = f32[64,2,1024]{2,1,0:T(2,128)S(1)} async-done(((f32[64,2,1024]{2,1,0:T(2,128)}), f32[64,2,1024]{2,1,0:T(2,128)S(1)}, u32[]{:S(2)}, u32[]{:S(2)}) %all-to-all-start.2) | async-done | bytes 524320 | tf_op jit(solution)/shard_map/all_to_all | solution.py:172
  216.5 0.8 copy.20
  (34 shorter events, 2.7 us)
Async XLA Ops:
  19.4 29.2 %collective-permute-start.3 = (bf16[2048,512]{1,0:T(8,128)(2,1)S(1)}, bf16[2048,512]{1,0:T(8,128)(2,1)S(1)}, u32[]{:S(2)}, u32[]{:S(2)}) collective-permute-start(bf16[2048,512]{1,0:T(8,128)(2,1)S(1)} %get-tuple-element.11), channel_id=1, source_target_pairs={{1,0},{2,1},{3,2},{4,3},{5,4},{6,5},{7,6},{8,7},{9,8},{10,9},{11,1... | collective-permute-start | bytes 6291464 | tf_op jit(solution)/shard_map/ppermute | solution.py:39
  23.4 28.8 %collective-permute-start.2 = (bf16[2048,512]{1,0:T(8,128)(2,1)S(1)}, bf16[2048,512]{1,0:T(8,128)(2,1)S(1)}, u32[]{:S(2)}, u32[]{:S(2)}) collective-permute-start(bf16[2048,512]{1,0:T(8,128)(2,1)S(1)} %get-tuple-element.10), channel_id=1, source_target_pairs={{0,1},{1,2},{2,3},{3,4},{4,5},{5,6},{6,7},{7,8},{8,9},{9,10},{10,1... | collective-permute-start | bytes 6291464 | tf_op jit(solution)/shard_map/ppermute | solution.py:37
  58.9 5.4 %copy-start.2 = (s32[1024]{0:T(1024)S(1)}, s32[1024]{0:T(1024)}, u32[]{:S(2)}) copy-start(s32[1024]{0:T(1024)} %param.9) | copy-start | bytes 12292
  58.9 5.4 %copy-start.1 = (s32[1024]{0:T(1024)S(1)}, s32[1024]{0:T(1024)}, u32[]{:S(2)}) copy-start(s32[1024]{0:T(1024)} %param.10) | copy-start | bytes 12292
  58.9 57.8 %all-to-all-start.1 = ((f32[4,256,1536]{2,1,0:T(8,128)}), f32[4,256,1536]{2,1,0:T(8,128)}, u32[]{:S(2)}, u32[]{:S(2)}) async-start(f32[4,256,1536]{2,1,0:T(8,128)} %bitcast.17), calls=%async_computation.1 | async-start | bytes 12582912 | tf_op jit(solution)/shard_map/all_to_all | solution.py:54
  64.3 7.4 %collective-permute-start.1 = (bf16[2,512]{1,0:T(2,128)(2,1)S(1)}, bf16[2,512]{1,0:T(2,128)(2,1)S(1)}, u32[]{:S(2)}, u32[]{:S(2)}) collective-permute-start(bf16[2,512]{1,0:T(2,128)(2,1)S(1)} %get-tuple-element.15), channel_id=1, source_target_pairs={{1,0},{2,1},{3,2},{4,3},{5,4},{6,5},{7,6},{8,7},{9,8},{10,9},{11,1... | collective-permute-start | bytes 6152 | tf_op jit(solution)/shard_map/ppermute | solution.py:39
  66.3 5.5 %collective-permute-start = (bf16[2,512]{1,0:T(2,128)(2,1)S(1)}, bf16[2,512]{1,0:T(2,128)(2,1)S(1)}, u32[]{:S(2)}, u32[]{:S(2)}) collective-permute-start(bf16[2,512]{1,0:T(2,128)(2,1)S(1)} %get-tuple-element.14), channel_id=1, source_target_pairs={{0,1},{1,2},{2,3},{3,4},{4,5},{5,6},{6,7},{7,8},{8,9},{9,10},{10,1... | collective-permute-start | bytes 6152 | tf_op jit(solution)/shard_map/ppermute | solution.py:37
  120.2 11.6 %copy-start = (f32[1024]{0:T(1024)S(1)}, f32[1024]{0:T(1024)}, u32[]{:S(2)}) copy-start(f32[1024]{0:T(1024)} %param.11) | copy-start | bytes 12292
  179.0 15.2 %all-to-all-start.4 = ((f32[64,1,261]{2,1,0:T(1,128)}), f32[64,1,261]{2,1,0:T(1,128)S(1)}, u32[]{:S(2)}, u32[]{:S(2)}) async-start(f32[64,1,261]{2,1,0:T(1,128)} %broadcast_in_dim.12), calls=%async_computation.4 | async-start | bytes 196608 | tf_op jit(solution)/shard_map/all_to_all | solution.py:11
  194.2 22.3 %all-to-all-start.2 = ((f32[64,2,1024]{2,1,0:T(2,128)}), f32[64,2,1024]{2,1,0:T(2,128)S(1)}, u32[]{:S(2)}, u32[]{:S(2)}) async-start(f32[64,2,1024]{2,1,0:T(2,128)} %all_to_all.33), calls=%async_computation.2 | async-start | bytes 1048576 | tf_op jit(solution)/shard_map/all_to_all | solution.py:172
where the time goes:
time: 218 us; the launch traced here: 217 us
  waiting for transfers between devices  92.3 us (42%)
  blocking collectives  62.4 us (29%)
  starting transfers between devices  27 us (12%)
  other arithmetic  18.8 us (9%)
  matrix products  9.47 us (4%)
  local copies, waits for them, and re-layouts  6.39 us (3%)
    all_to_all x1, waiting for transfers between devices, sum_at_owner(): lax.all_to_all(pieces, axis, split_axis=0, concat_axis=0, tiled=True)  44.8 us
    all_to_all x1, blocking collectives, sum_at_owner(): lax.all_to_all(pieces, axis, split_axis=0, concat_axis=0, tiled=True)  43.4 us
    ppermute x2, waiting for transfers between devices, extended(): lax.ppermute(head, axis, [((i + 1) % count, i) for i in range(ends)])  22.2 us
    all_to_all x1, waiting for transfers between devices, body(): lax.all_to_all(scores, 'snp', split_axis=0, concat_axis=1, tiled=True)  15.6 us
    all_gather x1, blocking collectives, body(): scores = lax.all_gather(part_scores, 'samp', axis=1, tiled=True)  9.9 us
    all_to_all x1, waiting for transfers between devices, from_everyone(): lax.all_to_all(jnp.broadcast_to(array[None], (size, *array.shape)), axis,...  9.6 us
    all_to_all x1, blocking collectives, from_everyone(): lax.all_to_all(jnp.broadcast_to(array[None], (size, *array.shape)), axis,...  9.1 us
    dot_general x4, matrix products, tile_piece(): lax.dot_general(rows_z, cols_z, (((0,), (0,)), ((), ())), preferred_eleme...  7.24 us
  transfers between devices with their start and end apart: 7, of which 4 were waited for; matrix products, arithmetic and copies ran while one was open for 3% of the time, Pallas kernels for 0%

commit v1 on v0

--- a/solution.py
+++ b/solution.py
@@ -154,7 +154,9 @@
         precision=lax.Precision.HIGHEST,
         preferred_element_type=jnp.float32,
     )
-    scores = lax.all_gather(part_scores, "samp", axis=1, tiled=True)
+    scores = jnp.concatenate(
+        lax.all_to_all(jnp.stack([part_scores] * lax.axis_size("samp")), "samp", 0, 0), axis=1
+    )
     weights = 1.0 / jnp.sum(scores, 0)
     weighted = scores * weights[None, :]
     gram_part = lax.dot_general(

time: 218 us -> 220 us (level)
  blocking collectives: 62.4 us -> 51.2 us
  waiting for transfers between devices: 92.3 us -> 100 us
  starting transfers between devices: 27 us -> 30.5 us
    all_gather x1 -> x0, blocking collectives: 9.9 us -> none  [body(): scores = lax.all_gather(part_scores, 'samp', axis=1, tiled=True)]
    all_to_all x0 -> x1, waiting for transfers between devices: none -> 6.88 us  [body(): lax.all_to_all(jnp.stack([part_scores] * lax.axis_size('samp')), 'samp',...]
    all_to_all x0 -> x1, starting transfers between devices: none -> 3.47 us  [body(): lax.all_to_all(jnp.stack([part_scores] * lax.axis_size('samp')), 'samp',...]
  transfers between devices with their start and end apart: 7 -> 8, of which waited for: 4 -> 5; matrix products, arithmetic and copies ran while one was open for 3% -> 4% of each run, Pallas kernels for 0% -> 0%
where the time goes in v1:
time: 220 us; the launch traced here: 219 us
  waiting for transfers between devices  100 us (45%)
  blocking collectives  51.2 us (23%)
  starting transfers between devices  30.5 us (14%)
  other arithmetic  19.4 us (9%)
  matrix products  9.48 us (4%)
  local copies, waits for them, and re-layouts  7.72 us (4%)
    all_to_all x1, waiting for transfers between devices, sum_at_owner(): lax.all_to_all(pieces, axis, split_axis=0, concat_axis=0, tiled=True)  46.2 us
    all_to_all x1, blocking collectives, sum_at_owner(): lax.all_to_all(pieces, axis, split_axis=0, concat_axis=0, tiled=True)  42.1 us
    ppermute x2, waiting for transfers between devices, extended(): lax.ppermute(head, axis, [((i + 1) % count, i) for i in range(ends)])  22.2 us
    all_to_all x1, waiting for transfers between devices, body(): lax.all_to_all(scores, 'snp', split_axis=0, concat_axis=1, tiled=True)  15.6 us
    all_to_all x1, waiting for transfers between devices, from_everyone(): lax.all_to_all(jnp.broadcast_to(array[None], (size, *array.shape)), axis,...  9.11 us
    all_to_all x1, blocking collectives, from_everyone(): lax.all_to_all(jnp.broadcast_to(array[None], (size, *array.shape)), axis,...  9.1 us
    dot_general x4, matrix products, tile_piece(): lax.dot_general(rows_z, cols_z, (((0,), (0,)), ((), ())), preferred_eleme...  7.24 us
    all_to_all x1, waiting for transfers between devices, body(): lax.all_to_all(jnp.stack([part_scores] * lax.axis_size('samp')), 'samp',...  6.88 us
  transfers between devices with their start and end apart: 8, of which 5 were waited for; matrix products, arithmetic and copies ran while one was open for 4% of the time, Pallas kernels for 0%

profile of v1, /device:TPU:1, one launch (start us, length us, event | category | flops | bytes accessed | tf_op | source)
XLA Modules:
  0.0 219.3 jit_solution(11893370944194334226)
XLA Ops:
  0.6 4.5 %convert_reduce_fusion = (f32[1024]{0:T(1024)S(1)}, f32[1024]{0:T(1024)S(1)}) fusion(s32[2048,1024]{1,0:T(8,128)} %param.6), kind=kLoop, calls=%fused_computation.2 | loop fusion | flops 8386560 | bytes 8396800 | tf_op jit(solution)/shard_map/reduce_sum | solution.py:97
  5.2 9.1 %all_to_all.50 = f32[4,1,2048]{2,1,0:T(1,128)S(1)} all-to-all(f32[4,1,2048]{2,1,0:T(1,128)S(1)} %broadcast_in_dim.9), channel_id=1, replica_groups=mesh['samp'=4,'snp'=64] {'samp'}, dimensions={0} | all-to-all | bytes 65536 | tf_op jit(solution)/shard_map/all_to_all | solution.py:11
  14.4 4.7 %multiply_convert_fusion = bf16[2048,1024]{1,0:T(8,128)(2,1)S(1)} fusion(s32[2048,1024]{1,0:T(8,128)} %param.6, f32[1024]{0:T(1024)S(1)} %get-tuple-element.17, f32[1024]{0:T(1024)S(1)} %get-tuple-element.16), kind=kLoop, calls=%fused_computation | loop fusion | flops 8388608 | bytes 12591104 | tf_op jit(solution)/shard_map/convert_element_type | solution.py:101
  19.4 4.0 %collective-permute-start.3 = (bf16[2048,512]{1,0:T(8,128)(2,1)S(1)}, bf16[2048,512]{1,0:T(8,128)(2,1)S(1)}, u32[]{:S(2)}, u32[]{:S(2)}) collective-permute-start(bf16[2048,512]{1,0:T(8,128)(2,1)S(1)} %get-tuple-element.11), channel_id=1, source_target_pairs={{1,0},{2,1},{3,2},{4,3},{5,4},{6,5},{7,6},{8,7},{9,8},{10,9},{11,1... | collective-permute-start | bytes 6291464 | tf_op jit(solution)/shard_map/ppermute | solution.py:39
  23.4 3.0 %collective-permute-start.2 = (bf16[2048,512]{1,0:T(8,128)(2,1)S(1)}, bf16[2048,512]{1,0:T(8,128)(2,1)S(1)}, u32[]{:S(2)}, u32[]{:S(2)}) collective-permute-start(bf16[2048,512]{1,0:T(8,128)(2,1)S(1)} %get-tuple-element.10), channel_id=1, source_target_pairs={{0,1},{1,2},{2,3},{3,4},{4,5},{5,6},{6,7},{7,8},{8,9},{9,10},{10,1... | collective-permute-start | bytes 6291464 | tf_op jit(solution)/shard_map/ppermute | solution.py:37
  26.4 22.2 %collective-permute-done.3 = bf16[2048,512]{1,0:T(8,128)(2,1)S(1)} collective-permute-done((bf16[2048,512]{1,0:T(8,128)(2,1)S(1)}, bf16[2048,512]{1,0:T(8,128)(2,1)S(1)}, u32[]{:S(2)}, u32[]{:S(2)}) %collective-permute-start.3) | collective-permute-done | bytes 2097184 | tf_op jit(solution)/shard_map/ppermute | solution.py:39
  48.6 1.8 fusion
  50.4 1.8 fusion.1
  52.2 1.8 fusion.2
  54.0 1.8 fusion.3
  55.9 3.0 %pad_maximum_fusion.2 = f32[1024,1536]{1,0:T(8,128)} fusion(f32[256,1536]{1,0:T(8,128)S(1)} %fusion, f32[256,1536]{1,0:T(8,128)S(1)} %fusion.1, f32[256,1536]{1,0:T(8,128)S(1)} %fusion.2, f32[256,1536]{1,0:T(8,128)S(1)} %fusion.3), kind=kLoop, calls=%fused_computation.5 | loop fusion | flops 4718592 | bytes 12582912 | tf_op jit(solution)/shard_map/concatenate | solution.py:124
  58.9 5.4 %all-to-all-start.1 = ((f32[4,256,1536]{2,1,0:T(8,128)}), f32[4,256,1536]{2,1,0:T(8,128)}, u32[]{:S(2)}, u32[]{:S(2)}) async-start(f32[4,256,1536]{2,1,0:T(8,128)} %bitcast.28), calls=%async_computation.1 | async-start | bytes 12582912 | tf_op jit(solution)/shard_map/all_to_all | solution.py:54
  64.3 1.9 collective-permute-start.1
  66.3 3.8 %collective-permute-start = (bf16[2,512]{1,0:T(2,128)(2,1)S(1)}, bf16[2,512]{1,0:T(2,128)(2,1)S(1)}, u32[]{:S(2)}, u32[]{:S(2)}) collective-permute-start(bf16[2,512]{1,0:T(2,128)(2,1)S(1)} %get-tuple-element.14), channel_id=1, source_target_pairs={{0,1},{1,2},{2,3},{3,4},{4,5},{5,6},{6,7},{7,8},{8,9},{9,10},{10,1... | collective-permute-start | bytes 6152 | tf_op jit(solution)/shard_map/ppermute | solution.py:37
  70.2 0.8 dynamic_slice.38
  71.0 0.8 dynamic_slice.37
  71.8 46.2 %all-to-all-done.1 = f32[4,256,1536]{2,1,0:T(8,128)} async-done(((f32[4,256,1536]{2,1,0:T(8,128)}), f32[4,256,1536]{2,1,0:T(8,128)}, u32[]{:S(2)}, u32[]{:S(2)}) %all-to-all-start.1) | async-done | bytes 6291488 | tf_op jit(solution)/shard_map/all_to_all | solution.py:54
  118.0 3.6 %reduce_sum.93 = f32[256,1536]{1,0:T(8,128)S(1)} reduce(f32[4,256,1536]{2,1,0:T(8,128)} %all-to-all-done.1, f32[]{:T(128)} %constant.123.clone.1), dimensions={0}, to_apply=%region_3.4 | reduce | flops 1179648 | bytes 7864324 | tf_op jit(solution)/shard_map/reduce_sum | solution.py:55
  121.6 1.6 fusion.4
  123.2 0.8 stack.37
  124.1 3.5 %all-to-all-start.2 = ((f32[4,128,256]{2,1,0:T(8,128)}), f32[4,128,256]{2,1,0:T(8,128)S(1)}, u32[]{:S(2)}, u32[]{:S(2)}) async-start(f32[4,128,256]{2,1,0:T(8,128)} %stack.37), calls=%async_computation.2 | async-start | bytes 1048576 | tf_op jit(solution)/shard_map/all_to_all | solution.py:158
  127.6 6.9 %all-to-all-done.2 = f32[4,128,256]{2,1,0:T(8,128)S(1)} async-done(((f32[4,128,256]{2,1,0:T(8,128)}), f32[4,128,256]{2,1,0:T(8,128)S(1)}, u32[]{:S(2)}, u32[]{:S(2)}) %all-to-all-start.2) | async-done | bytes 524320 | tf_op jit(solution)/shard_map/all_to_all | solution.py:158
  136.5 1.4 concatenate.24
  138.2 42.1 %all_to_all.51 = f32[64,1,261]{2,1,0:T(1,128)S(1)} all-to-all(f32[64,1,261]{2,1,0:T(1,128)S(1)} %all_to_all.41), channel_id=1, replica_groups=mesh['samp'=4,'snp'=64] {'snp'}, dimensions={0} | all-to-all | bytes 133632 | tf_op jit(solution)/shard_map/all_to_all | solution.py:54
  180.4 0.7 broadcast_in_dim.12
  181.1 4.4 %all-to-all-start.5 = ((f32[64,1,261]{2,1,0:T(1,128)}), f32[64,1,261]{2,1,0:T(1,128)S(1)}, u32[]{:S(2)}, u32[]{:S(2)}) async-start(f32[64,1,261]{2,1,0:T(1,128)} %broadcast_in_dim.12), calls=%async_computation.5 | async-start | bytes 196608 | tf_op jit(solution)/shard_map/all_to_all | solution.py:11
  185.9 1.2 all_to_all.37
  187.1 9.1 %all-to-all-done.5 = f32[64,1,261]{2,1,0:T(1,128)S(1)} async-done(((f32[64,1,261]{2,1,0:T(1,128)}), f32[64,1,261]{2,1,0:T(1,128)S(1)}, u32[]{:S(2)}, u32[]{:S(2)}) %all-to-all-start.5) | async-done | bytes 66848 | tf_op jit(solution)/shard_map/all_to_all | solution.py:11
  196.2 4.5 %all-to-all-start.3 = ((f32[64,2,1024]{2,1,0:T(2,128)}), f32[64,2,1024]{2,1,0:T(2,128)S(1)}, u32[]{:S(2)}, u32[]{:S(2)}) async-start(f32[64,2,1024]{2,1,0:T(2,128)} %all_to_all.37), calls=%async_computation.3 | async-start | bytes 1048576 | tf_op jit(solution)/shard_map/all_to_all | solution.py:174
  202.2 0.6 fusion.35
  202.8 15.6 %all-to-all-done.3 = f32[64,2,1024]{2,1,0:T(2,128)S(1)} async-done(((f32[64,2,1024]{2,1,0:T(2,128)}), f32[64,2,1024]{2,1,0:T(2,128)S(1)}, u32[]{:S(2)}, u32[]{:S(2)}) %all-to-all-start.3) | async-done | bytes 524320 | tf_op jit(solution)/shard_map/all_to_all | solution.py:174
  218.5 0.8 copy.21
  (40 shorter events, 4.9 us)
Async XLA Ops:
  19.4 29.2 %collective-permute-start.3 = (bf16[2048,512]{1,0:T(8,128)(2,1)S(1)}, bf16[2048,512]{1,0:T(8,128)(2,1)S(1)}, u32[]{:S(2)}, u32[]{:S(2)}) collective-permute-start(bf16[2048,512]{1,0:T(8,128)(2,1)S(1)} %get-tuple-element.11), channel_id=1, source_target_pairs={{1,0},{2,1},{3,2},{4,3},{5,4},{6,5},{7,6},{8,7},{9,8},{10,9},{11,1... | collective-permute-start | bytes 6291464 | tf_op jit(solution)/shard_map/ppermute | solution.py:39
  23.4 28.8 %collective-permute-start.2 = (bf16[2048,512]{1,0:T(8,128)(2,1)S(1)}, bf16[2048,512]{1,0:T(8,128)(2,1)S(1)}, u32[]{:S(2)}, u32[]{:S(2)}) collective-permute-start(bf16[2048,512]{1,0:T(8,128)(2,1)S(1)} %get-tuple-element.10), channel_id=1, source_target_pairs={{0,1},{1,2},{2,3},{3,4},{4,5},{5,6},{6,7},{7,8},{8,9},{9,10},{10,1... | collective-permute-start | bytes 6291464 | tf_op jit(solution)/shard_map/ppermute | solution.py:37
  58.9 5.4 %copy-start.2 = (s32[1024]{0:T(1024)S(1)}, s32[1024]{0:T(1024)}, u32[]{:S(2)}) copy-start(s32[1024]{0:T(1024)} %param.9) | copy-start | bytes 12292
  58.9 5.4 %copy-start.1 = (s32[1024]{0:T(1024)S(1)}, s32[1024]{0:T(1024)}, u32[]{:S(2)}) copy-start(s32[1024]{0:T(1024)} %param.10) | copy-start | bytes 12292
  58.9 59.2 %all-to-all-start.1 = ((f32[4,256,1536]{2,1,0:T(8,128)}), f32[4,256,1536]{2,1,0:T(8,128)}, u32[]{:S(2)}, u32[]{:S(2)}) async-start(f32[4,256,1536]{2,1,0:T(8,128)} %bitcast.28), calls=%async_computation.1 | async-start | bytes 12582912 | tf_op jit(solution)/shard_map/all_to_all | solution.py:54
  64.3 7.4 %collective-permute-start.1 = (bf16[2,512]{1,0:T(2,128)(2,1)S(1)}, bf16[2,512]{1,0:T(2,128)(2,1)S(1)}, u32[]{:S(2)}, u32[]{:S(2)}) collective-permute-start(bf16[2,512]{1,0:T(2,128)(2,1)S(1)} %get-tuple-element.15), channel_id=1, source_target_pairs={{1,0},{2,1},{3,2},{4,3},{5,4},{6,5},{7,6},{8,7},{9,8},{10,9},{11,1... | collective-permute-start | bytes 6152 | tf_op jit(solution)/shard_map/ppermute | solution.py:39
  66.3 5.5 %collective-permute-start = (bf16[2,512]{1,0:T(2,128)(2,1)S(1)}, bf16[2,512]{1,0:T(2,128)(2,1)S(1)}, u32[]{:S(2)}, u32[]{:S(2)}) collective-permute-start(bf16[2,512]{1,0:T(2,128)(2,1)S(1)} %get-tuple-element.14), channel_id=1, source_target_pairs={{0,1},{1,2},{2,3},{3,4},{4,5},{5,6},{6,7},{7,8},{8,9},{9,10},{10,1... | collective-permute-start | bytes 6152 | tf_op jit(solution)/shard_map/ppermute | solution.py:37
  121.6 6.0 %copy-start = (f32[1024]{0:T(1024)S(1)}, f32[1024]{0:T(1024)}, u32[]{:S(2)}) copy-start(f32[1024]{0:T(1024)} %param.11) | copy-start | bytes 12292
  124.1 10.4 %all-to-all-start.2 = ((f32[4,128,256]{2,1,0:T(8,128)}), f32[4,128,256]{2,1,0:T(8,128)S(1)}, u32[]{:S(2)}, u32[]{:S(2)}) async-start(f32[4,128,256]{2,1,0:T(8,128)} %stack.37), calls=%async_computation.2 | async-start | bytes 1048576 | tf_op jit(solution)/shard_map/all_to_all | solution.py:158
  181.1 15.2 %all-to-all-start.5 = ((f32[64,1,261]{2,1,0:T(1,128)}), f32[64,1,261]{2,1,0:T(1,128)S(1)}, u32[]{:S(2)}, u32[]{:S(2)}) async-start(f32[64,1,261]{2,1,0:T(1,128)} %broadcast_in_dim.12), calls=%async_computation.5 | async-start | bytes 196608 | tf_op jit(solution)/shard_map/all_to_all | solution.py:11
  196.2 22.3 %all-to-all-start.3 = ((f32[64,2,1024]{2,1,0:T(2,128)}), f32[64,2,1024]{2,1,0:T(2,128)S(1)}, u32[]{:S(2)}, u32[]{:S(2)}) async-start(f32[64,2,1024]{2,1,0:T(2,128)} %all_to_all.37), calls=%async_computation.3 | async-start | bytes 1048576 | tf_op jit(solution)/shard_map/all_to_all | solution.py:174
